TPU v7x, 32 devices: a whole 2x2x4 slice. The times are simulated.
32 devices in a mesh: sky: 4 (over x, core), tm: 8 (over z, y).
Axes of the slice: x: 2, y: 2, z: 4, core: 2. Of those that a mesh axis runs over, the one named last changes fastest.
Arguments:
- attitude: float32 [4, 8, 512], P(None, 'tm', 'sky'), may hold values from -6 to 6
- slot_time: float32 [262144], P(('sky', 'tm')), may hold values from -1 to 1
- slot_parallax: float32 [262144], P(('sky', 'tm')), may hold values from -1 to 1
- slot_observed: float32 [262144], P(('sky', 'tm')), may hold values from -6 to 6
- slot_phase: float32 [262144], P(('sky', 'tm')), may hold values from 0 to 1
- slot_knot: int32 [262144], P(('sky', 'tm')), may hold values from 0 to 508
- block_source: int32 [8192], P(('sky', 'tm')), may hold values from 0 to 63
- block_count: int32 [8192], P(('sky', 'tm')), may hold values from 1 to 32
- prior: float32 [5, 256], P(None, ('sky', 'tm')), may hold values from 0.5 to 4
Outputs:
- update: float32 [5, 256], P(None, ('sky', 'tm'))
Inputs may be any that keep to these rules, and one draw needn't show every extreme that they name: The four knots from slot_knot on lie in the transit's time group of 512 knots. `block_source`: an index into the 64 sources of the block's own sky sector.
All inputs are finite; a program needn't handle non-finite values.
Results may differ from a plain program's by a relative error of at most 0.0003.
Values sent between devices are 32-bit elements; how exact they have to be, the bound alone decides.
A program may use at most 64 MiB of HBM per device.

v0:
```python
import math
import jax
import jax.numpy as jnp
from jax import lax
from jax.sharding import PartitionSpec as P

PAIR_LIST = [(i, j) for i in range(5) for j in range(i, 5)]


def spline_quat(table, knot, phase):
    total = knot.shape[0]
    width = table.shape[1]
    step = math.gcd(total, 512)
    knot_rows = knot.reshape(total // step, step)
    phase_rows = phase.reshape(total // step, step)
    positions = jnp.arange(width, dtype=jnp.int32)

    def one_block(items):
        knot_here, phase_here = items
        weights = [
            (1.0 - phase_here) ** 3 / 6.0,
            (3.0 * phase_here**3 - 6.0 * phase_here**2 + 4.0) / 6.0,
            (-3.0 * phase_here**3 + 3.0 * phase_here**2 + 3.0 * phase_here + 1.0) / 6.0,
            phase_here**3 / 6.0,
        ]
        offset = positions[None, :] - knot_here[:, None]
        spread = jnp.zeros((step, width), jnp.float32)
        for i in range(4):
            spread = jnp.where(offset == i, weights[i][:, None], spread)
        return lax.dot_general(
            table,
            spread,
            (((1,), (1,)), ((), ())),
            precision=lax.Precision.HIGHEST,
            preferred_element_type=jnp.float32,
        )

    quat = lax.map(one_block, (knot_rows, phase_rows))
    return jnp.transpose(quat, (1, 0, 2)).reshape(4, total)


def block_sums(table, knot, phase, time, parallax, observed, count):
    quat = spline_quat(table, knot, phase)
    cross = quat[0] * quat[0] + quat[1] * quat[1] - quat[2] * quat[2] - quat[3] * quat[3]
    along = 2.0 * (quat[1] * quat[2] + quat[0] * quat[3])
    tilt = 2.0 * (quat[1] * quat[3] - quat[0] * quat[2])
    design = [cross, along, parallax, time * cross, time * along]
    residual = observed - tilt
    rows = [design[i] * design[j] for i, j in PAIR_LIST] + [design[i] * residual for i in range(5)]
    stacked = jnp.stack(rows)
    blocks = count.shape[0]
    stacked = stacked.reshape(20, blocks, -1)
    live = (jnp.arange(stacked.shape[2], dtype=jnp.int32)[None, :] < count[:, None]).astype(
        stacked.dtype
    )
    return jnp.sum(stacked * live[None], axis=2)


def source_sums(sums, block_source, sector_sources):
    blocks = block_source.shape[0]
    step = math.gcd(blocks, 512)
    source_rows = block_source.reshape(blocks // step, step)
    sum_rows = jnp.transpose(sums.reshape(20, blocks // step, step), (1, 0, 2))
    positions = jnp.arange(sector_sources, dtype=jnp.int32)

    def add_block(carry, items):
        source_here, sums_here = items
        member = (source_here[:, None] == positions[None, :]).astype(jnp.float32)
        return (
            carry
            + jnp.dot(
                sums_here,
                member,
                precision=lax.Precision.HIGHEST,
                preferred_element_type=jnp.float32,
            ),
            None,
        )

    start = jnp.zeros((20, sector_sources), jnp.float32)
    total, _ = lax.scan(add_block, start, (source_rows, sum_rows))
    return total


def solve_normals(normal, prior):
    entry = {}
    for index, pair in enumerate(PAIR_LIST):
        entry[pair[1], pair[0]] = normal[index]
    for i in range(5):
        entry[i, i] = entry[i, i] + prior[i]
    lower = {}
    for col in range(5):
        pivot = entry[col, col]
        for k in range(col):
            pivot = pivot - lower[col, k] * lower[col, k]
        root = jnp.sqrt(pivot)
        lower[col, col] = root
        for row in range(col + 1, 5):
            value = entry[row, col]
            for k in range(col):
                value = value - lower[row, k] * lower[col, k]
            lower[row, col] = value / root
    forward = []
    for i in range(5):
        value = normal[15 + i]
        for k in range(i):
            value = value - lower[i, k] * forward[k]
        forward.append(value / lower[i, i])
    result = [None] * 5
    for i in range(4, -1, -1):
        value = forward[i]
        for k in range(i + 1, 5):
            value = value - lower[k, i] * result[k]
        result[i] = value / lower[i, i]
    return jnp.stack(result)


def on_device(
    attitude,
    slot_time,
    slot_parallax,
    slot_observed,
    slot_phase,
    slot_knot,
    block_source,
    block_count,
    prior,
):
    group = lax.all_gather(attitude, "sky", axis=2, tiled=True)
    table = group[:, 0, :]
    sums = block_sums(
        table, slot_knot, slot_phase, slot_time, slot_parallax, slot_observed, block_count
    )
    owned = prior.shape[1]
    sector_sources = owned * lax.axis_size("tm")
    partial_value = source_sums(sums, block_source, sector_sources)
    total = lax.psum(partial_value, "tm")
    normal = lax.dynamic_slice_in_dim(total, lax.axis_index("tm") * owned, owned, 1)
    return solve_normals(normal, prior)


def solution(mesh):
    in_specs = (
        P(None, "tm", "sky"),
        P(("sky", "tm")),
        P(("sky", "tm")),
        P(("sky", "tm")),
        P(("sky", "tm")),
        P(("sky", "tm")),
        P(("sky", "tm")),
        P(("sky", "tm")),
        P(None, ("sky", "tm")),
    )
    out_specs = P(None, ("sky", "tm"))
    return jax.shard_map(
        on_device, mesh=mesh, in_specs=in_specs, out_specs=out_specs, check_vma=False
    )
```

profile of v0, /device:TPU:0, one launch (start us, length us, event | category | flops | bytes accessed | tf_op | source)
XLA Modules:
  0.0 77.9 jit_solution(18191354367063263991)
XLA Ops:
  0.0 0.8 reshape.292
  0.8 0.7 copy-done.4
  1.5 6.2 %all_gather.3 = f32[4,1,512]{2,0,1:T(4,128)S(1)} all-gather(f32[4,1,128]{2,0,1:T(4,128)S(1)} %bitcast.33), channel_id=1, replica_groups=mesh['sky'=4,'tm'=8] {'sky'}, dimensions={2}, use_global_device_ids=true | all-gather | bytes 10240 | tf_op jit(solution)/shard_map/all_gather | solution.py:129
  7.6 22.9 %while.3 = (s32[]{:T(128)}, f32[16,4,512]{2,1,0:T(4,128)S(1)}, s32[16,512]{1,0:T(8,128)S(1)}, f32[16,512]{1,0:T(8,128)S(1)}, f32[4,512]{1,0:T(4,128)S(1)}, /*index=5*/s32[]{:T(128)}) while((s32[]{:T(128)}, f32[16,4,512]{2,1,0:T(4,128)S(1)}, s32[16,512]{1,0:T(8,128)S(1)}, f32[16,512]{1,0:T(8,128)S(1)}, f32[4,512]{1,0:T(4,128)S(1)}, ...), condition=%wide.region_1.2_spmd.clone, body=%wide.region_0.1_spmd.clone.sunk | while | flops 14951938 | bytes 45145 | solution.py:38
  7.6 1.4 %fusion.59 = f32[16,4,512]{2,1,0:T(4,128)S(1)} fusion(f32[16,4,512]{2,1,0:T(4,128)S(1)} %get-tuple-element.192, s32[]{:T(128)S(6)} %copy.59, f32[4,512]{1,0:T(4,128)S(1)} %get-tuple-element.201, f32[512]{0:T(512)S(1)} %get-tuple-element.181, f32[512]{0:T(512)S(1)} %get-tuple-element.182, f32[512]{0:T(512)S(1)} %get-tuple-element.183, ...), kind=kOutput, calls=%fused_computation.2.clone.1 | convolution fusion | flops 14942208 | bytes 26628 | tf_op jit(solution)/shard_map/while/body/eval_jaxpr/dot_general | solution.py:30
  9.1 1.4 %fusion.59 = f32[16,4,512]{2,1,0:T(4,128)S(1)} fusion(f32[16,4,512]{2,1,0:T(4,128)S(1)} %get-tuple-element.192, s32[]{:T(128)S(6)} %copy.59, f32[4,512]{1,0:T(4,128)S(1)} %get-tuple-element.201, f32[512]{0:T(512)S(1)} %get-tuple-element.181, f32[512]{0:T(512)S(1)} %get-tuple-element.182, f32[512]{0:T(512)S(1)} %get-tuple-element.183, ...), kind=kOutput, calls=%fused_computation.2.clone.1 | convolution fusion | flops 14942208 | bytes 26628 | tf_op jit(solution)/shard_map/while/body/eval_jaxpr/dot_general | solution.py:30
  10.5 1.4 %fusion.59 = f32[16,4,512]{2,1,0:T(4,128)S(1)} fusion(f32[16,4,512]{2,1,0:T(4,128)S(1)} %get-tuple-element.192, s32[]{:T(128)S(6)} %copy.59, f32[4,512]{1,0:T(4,128)S(1)} %get-tuple-element.201, f32[512]{0:T(512)S(1)} %get-tuple-element.181, f32[512]{0:T(512)S(1)} %get-tuple-element.182, f32[512]{0:T(512)S(1)} %get-tuple-element.183, ...), kind=kOutput, calls=%fused_computation.2.clone.1 | convolution fusion | flops 14942208 | bytes 26628 | tf_op jit(solution)/shard_map/while/body/eval_jaxpr/dot_general | solution.py:30
  12.0 1.4 %fusion.59 = f32[16,4,512]{2,1,0:T(4,128)S(1)} fusion(f32[16,4,512]{2,1,0:T(4,128)S(1)} %get-tuple-element.192, s32[]{:T(128)S(6)} %copy.59, f32[4,512]{1,0:T(4,128)S(1)} %get-tuple-element.201, f32[512]{0:T(512)S(1)} %get-tuple-element.181, f32[512]{0:T(512)S(1)} %get-tuple-element.182, f32[512]{0:T(512)S(1)} %get-tuple-element.183, ...), kind=kOutput, calls=%fused_computation.2.clone.1 | convolution fusion | flops 14942208 | bytes 26628 | tf_op jit(solution)/shard_map/while/body/eval_jaxpr/dot_general | solution.py:30
  13.4 1.4 %fusion.59 = f32[16,4,512]{2,1,0:T(4,128)S(1)} fusion(f32[16,4,512]{2,1,0:T(4,128)S(1)} %get-tuple-element.192, s32[]{:T(128)S(6)} %copy.59, f32[4,512]{1,0:T(4,128)S(1)} %get-tuple-element.201, f32[512]{0:T(512)S(1)} %get-tuple-element.181, f32[512]{0:T(512)S(1)} %get-tuple-element.182, f32[512]{0:T(512)S(1)} %get-tuple-element.183, ...), kind=kOutput, calls=%fused_computation.2.clone.1 | convolution fusion | flops 14942208 | bytes 26628 | tf_op jit(solution)/shard_map/while/body/eval_jaxpr/dot_general | solution.py:30
  14.8 1.4 %fusion.59 = f32[16,4,512]{2,1,0:T(4,128)S(1)} fusion(f32[16,4,512]{2,1,0:T(4,128)S(1)} %get-tuple-element.192, s32[]{:T(128)S(6)} %copy.59, f32[4,512]{1,0:T(4,128)S(1)} %get-tuple-element.201, f32[512]{0:T(512)S(1)} %get-tuple-element.181, f32[512]{0:T(512)S(1)} %get-tuple-element.182, f32[512]{0:T(512)S(1)} %get-tuple-element.183, ...), kind=kOutput, calls=%fused_computation.2.clone.1 | convolution fusion | flops 14942208 | bytes 26628 | tf_op jit(solution)/shard_map/while/body/eval_jaxpr/dot_general | solution.py:30
  16.3 1.4 %fusion.59 = f32[16,4,512]{2,1,0:T(4,128)S(1)} fusion(f32[16,4,512]{2,1,0:T(4,128)S(1)} %get-tuple-element.192, s32[]{:T(128)S(6)} %copy.59, f32[4,512]{1,0:T(4,128)S(1)} %get-tuple-element.201, f32[512]{0:T(512)S(1)} %get-tuple-element.181, f32[512]{0:T(512)S(1)} %get-tuple-element.182, f32[512]{0:T(512)S(1)} %get-tuple-element.183, ...), kind=kOutput, calls=%fused_computation.2.clone.1 | convolution fusion | flops 14942208 | bytes 26628 | tf_op jit(solution)/shard_map/while/body/eval_jaxpr/dot_general | solution.py:30
  17.7 1.4 %fusion.59 = f32[16,4,512]{2,1,0:T(4,128)S(1)} fusion(f32[16,4,512]{2,1,0:T(4,128)S(1)} %get-tuple-element.192, s32[]{:T(128)S(6)} %copy.59, f32[4,512]{1,0:T(4,128)S(1)} %get-tuple-element.201, f32[512]{0:T(512)S(1)} %get-tuple-element.181, f32[512]{0:T(512)S(1)} %get-tuple-element.182, f32[512]{0:T(512)S(1)} %get-tuple-element.183, ...), kind=kOutput, calls=%fused_computation.2.clone.1 | convolution fusion | flops 14942208 | bytes 26628 | tf_op jit(solution)/shard_map/while/body/eval_jaxpr/dot_general | solution.py:30
  19.1 1.4 %fusion.59 = f32[16,4,512]{2,1,0:T(4,128)S(1)} fusion(f32[16,4,512]{2,1,0:T(4,128)S(1)} %get-tuple-element.192, s32[]{:T(128)S(6)} %copy.59, f32[4,512]{1,0:T(4,128)S(1)} %get-tuple-element.201, f32[512]{0:T(512)S(1)} %get-tuple-element.181, f32[512]{0:T(512)S(1)} %get-tuple-element.182, f32[512]{0:T(512)S(1)} %get-tuple-element.183, ...), kind=kOutput, calls=%fused_computation.2.clone.1 | convolution fusion | flops 14942208 | bytes 26628 | tf_op jit(solution)/shard_map/while/body/eval_jaxpr/dot_general | solution.py:30
  20.6 1.4 %fusion.59 = f32[16,4,512]{2,1,0:T(4,128)S(1)} fusion(f32[16,4,512]{2,1,0:T(4,128)S(1)} %get-tuple-element.192, s32[]{:T(128)S(6)} %copy.59, f32[4,512]{1,0:T(4,128)S(1)} %get-tuple-element.201, f32[512]{0:T(512)S(1)} %get-tuple-element.181, f32[512]{0:T(512)S(1)} %get-tuple-element.182, f32[512]{0:T(512)S(1)} %get-tuple-element.183, ...), kind=kOutput, calls=%fused_computation.2.clone.1 | convolution fusion | flops 14942208 | bytes 26628 | tf_op jit(solution)/shard_map/while/body/eval_jaxpr/dot_general | solution.py:30
  22.0 1.4 %fusion.59 = f32[16,4,512]{2,1,0:T(4,128)S(1)} fusion(f32[16,4,512]{2,1,0:T(4,128)S(1)} %get-tuple-element.192, s32[]{:T(128)S(6)} %copy.59, f32[4,512]{1,0:T(4,128)S(1)} %get-tuple-element.201, f32[512]{0:T(512)S(1)} %get-tuple-element.181, f32[512]{0:T(512)S(1)} %get-tuple-element.182, f32[512]{0:T(512)S(1)} %get-tuple-element.183, ...), kind=kOutput, calls=%fused_computation.2.clone.1 | convolution fusion | flops 14942208 | bytes 26628 | tf_op jit(solution)/shard_map/while/body/eval_jaxpr/dot_general | solution.py:30
  23.4 1.4 %fusion.59 = f32[16,4,512]{2,1,0:T(4,128)S(1)} fusion(f32[16,4,512]{2,1,0:T(4,128)S(1)} %get-tuple-element.192, s32[]{:T(128)S(6)} %copy.59, f32[4,512]{1,0:T(4,128)S(1)} %get-tuple-element.201, f32[512]{0:T(512)S(1)} %get-tuple-element.181, f32[512]{0:T(512)S(1)} %get-tuple-element.182, f32[512]{0:T(512)S(1)} %get-tuple-element.183, ...), kind=kOutput, calls=%fused_computation.2.clone.1 | convolution fusion | flops 14942208 | bytes 26628 | tf_op jit(solution)/shard_map/while/body/eval_jaxpr/dot_general | solution.py:30
  24.9 1.4 %fusion.59 = f32[16,4,512]{2,1,0:T(4,128)S(1)} fusion(f32[16,4,512]{2,1,0:T(4,128)S(1)} %get-tuple-element.192, s32[]{:T(128)S(6)} %copy.59, f32[4,512]{1,0:T(4,128)S(1)} %get-tuple-element.201, f32[512]{0:T(512)S(1)} %get-tuple-element.181, f32[512]{0:T(512)S(1)} %get-tuple-element.182, f32[512]{0:T(512)S(1)} %get-tuple-element.183, ...), kind=kOutput, calls=%fused_computation.2.clone.1 | convolution fusion | flops 14942208 | bytes 26628 | tf_op jit(solution)/shard_map/while/body/eval_jaxpr/dot_general | solution.py:30
  26.3 1.4 %fusion.59 = f32[16,4,512]{2,1,0:T(4,128)S(1)} fusion(f32[16,4,512]{2,1,0:T(4,128)S(1)} %get-tuple-element.192, s32[]{:T(128)S(6)} %copy.59, f32[4,512]{1,0:T(4,128)S(1)} %get-tuple-element.201, f32[512]{0:T(512)S(1)} %get-tuple-element.181, f32[512]{0:T(512)S(1)} %get-tuple-element.182, f32[512]{0:T(512)S(1)} %get-tuple-element.183, ...), kind=kOutput, calls=%fused_computation.2.clone.1 | convolution fusion | flops 14942208 | bytes 26628 | tf_op jit(solution)/shard_map/while/body/eval_jaxpr/dot_general | solution.py:30
  27.7 1.4 %fusion.59 = f32[16,4,512]{2,1,0:T(4,128)S(1)} fusion(f32[16,4,512]{2,1,0:T(4,128)S(1)} %get-tuple-element.192, s32[]{:T(128)S(6)} %copy.59, f32[4,512]{1,0:T(4,128)S(1)} %get-tuple-element.201, f32[512]{0:T(512)S(1)} %get-tuple-element.181, f32[512]{0:T(512)S(1)} %get-tuple-element.182, f32[512]{0:T(512)S(1)} %get-tuple-element.183, ...), kind=kOutput, calls=%fused_computation.2.clone.1 | convolution fusion | flops 14942208 | bytes 26628 | tf_op jit(solution)/shard_map/while/body/eval_jaxpr/dot_general | solution.py:30
  29.2 1.4 %fusion.59 = f32[16,4,512]{2,1,0:T(4,128)S(1)} fusion(f32[16,4,512]{2,1,0:T(4,128)S(1)} %get-tuple-element.192, s32[]{:T(128)S(6)} %copy.59, f32[4,512]{1,0:T(4,128)S(1)} %get-tuple-element.201, f32[512]{0:T(512)S(1)} %get-tuple-element.181, f32[512]{0:T(512)S(1)} %get-tuple-element.182, f32[512]{0:T(512)S(1)} %get-tuple-element.183, ...), kind=kOutput, calls=%fused_computation.2.clone.1 | convolution fusion | flops 14942208 | bytes 26628 | tf_op jit(solution)/shard_map/while/body/eval_jaxpr/dot_general | solution.py:30
  30.5 0.4 multiply_reduce_fusion.1
  31.0 0.1 reshape.294
  31.2 0.1 reshape.295
  31.3 0.7 copy-done
  32.1 0.7 copy-done.1
  32.9 0.1 stack.65
  33.1 0.1 stack.66
  33.3 0.1 stack.67
  33.5 0.1 reshape.296
  33.6 0.1 stack.68
  33.8 0.1 stack.69
  34.0 0.1 stack.70
  34.2 0.1 stack.71
  34.4 0.1 stack.72
  34.5 0.1 stack.73
  34.7 0.1 stack.74
  34.9 0.1 stack.75
  36.2 0.7 copy-done.6
  36.8 0.1 multiply_reduce_fusion
  36.9 0.6 copy-done.7
  37.5 0.3 fusion.39
  37.9 37.9 %psum.7 = f32[20,64]{0,1:T(8,128)S(1)} all-reduce(f32[20,64]{0,1:T(8,128)S(1)} %fusion.39), channel_id=1, replica_groups=mesh['sky'=4,'tm'=8] {'tm'}, use_global_device_ids=true, to_apply=%region_3.4 | all-reduce | flops 1280 | bytes 10240 | tf_op jit(solution)/shard_map/psum | solution.py:137
  75.8 0.7 copy-done.5
  76.5 0.1 copy.54
  76.8 0.1 subtract_divide_fusion.7
  76.9 0.1 subtract_divide_fusion.4
  77.1 0.1 subtract_divide_fusion
  77.3 0.7 copy.50
  (117 shorter events, 3.2 us)
Async XLA Ops:
  0.0 0.8 copy-start.3
  0.8 0.7 copy-start.4
  31.3 0.8 copy-start
  31.3 0.8 %copy-start.2 = (f32[8192]{0:T(1024)S(1)}, f32[8192]{0:T(1024)}, u32[]{:S(2)}) copy-start(f32[8192]{0:T(1024)} %param.14) | copy-start | bytes 98308
  32.1 0.8 copy-start.1
  36.1 0.7 copy-start.6
  36.8 0.7 copy-start.7
  75.8 0.7 copy-start.5
where the time goes:
time: 78.4 us; the launch traced here: 77.9 us
  blocking collectives  44.1 us (56%)
  matrix products  22.3 us (28%)
  local copies, waits for them, and re-layouts  9.75 us (12%)
  other arithmetic  1.07 us (1%)
    psum x1, blocking collectives, on_device(): total = lax.psum(partial_value, 'tm')  37.9 us
    dot_general x16, matrix products, one_block(): lax.dot_general(table, spread, (((1,), (1,)), ((), ())), precision=lax.Pr...  22 us
    all_gather x1, blocking collectives, on_device(): group = lax.all_gather(attitude, 'sky', axis=2, tiled=True)  6.15 us
    unnamed x40, local copies, waits for them, and re-layouts  4.73 us
    another operation x35, local copies, waits for them, and re-layouts, block_sums(): stacked = jnp.stack(rows)  2.6 us

commit v1 on v0

--- a/solution.py
+++ b/solution.py
@@ -134,7 +134,10 @@
     owned = prior.shape[1]
     sector_sources = owned * lax.axis_size("tm")
     partial_value = source_sums(sums, block_source, sector_sources)
-    total = lax.psum(partial_value, "tm")
+    peers, total = (lax.axis_size("tm"), partial_value)
+    for far in [1 << k_2 for k_2 in range(peers.bit_length() - 1)]:
+        swap = [(i_2, i_2 ^ far) for i_2 in range(peers)]
+        total = total + lax.ppermute(total, "tm", swap)
     normal = lax.dynamic_slice_in_dim(total, lax.axis_index("tm") * owned, owned, 1)
     return solve_normals(normal, prior)
 

time: 78.4 us -> 51.2 us (0.65)
  blocking collectives: 44.1 us -> 6.15 us
  starting transfers between devices: 0 us -> 7.2 us
  waiting for transfers between devices: 0 us -> 5.02 us
  local copies, waits for them, and re-layouts: 9.75 us -> 8.47 us
    psum x1 -> x0, blocking collectives: 37.9 us -> none  [on_device(): total = lax.psum(partial_value, 'tm')]
    ppermute x0 -> x3, starting transfers between devices: none -> 7.2 us  [on_device(): total = total + lax.ppermute(total, 'tm', swap)]
    ppermute x0 -> x3, waiting for transfers between devices: none -> 5.02 us  [on_device(): total = total + lax.ppermute(total, 'tm', swap)]
    unnamed x40 -> x35, local copies, waits for them, and re-layouts: 4.73 us -> 3.41 us
  transfers between devices with their start and end apart: 0 -> 3, of which waited for: 0 -> 3; matrix products, arithmetic and copies ran while one was open for 0% -> 0% of each run, Pallas kernels for 0% -> 0%
where the time goes in v1:
time: 51.2 us; the launch traced here: 50.8 us
  matrix products  22.2 us (43%)
  local copies, waits for them, and re-layouts  8.47 us (17%)
  starting transfers between devices  7.2 us (14%)
  blocking collectives  6.15 us (12%)
  waiting for transfers between devices  5.02 us (10%)
  other arithmetic  0.97 us (2%)
    dot_general x16, matrix products, one_block(): lax.dot_general(table, spread, (((1,), (1,)), ((), ())), precision=lax.Pr...  22 us
    ppermute x3, starting transfers between devices, on_device(): total = total + lax.ppermute(total, 'tm', swap)  7.2 us
    all_gather x1, blocking collectives, on_device(): group = lax.all_gather(attitude, 'sky', axis=2, tiled=True)  6.15 us
    ppermute x3, waiting for transfers between devices, on_device(): total = total + lax.ppermute(total, 'tm', swap)  5.02 us
    unnamed x35, local copies, waits for them, and re-layouts  3.41 us
    another operation x35, local copies, waits for them, and re-layouts, block_sums(): stacked = jnp.stack(rows)  2.78 us
  transfers between devices with their start and end apart: 3, of which 3 were waited for; matrix products, arithmetic and copies ran while one was open for 0% of the time, Pallas kernels for 0%

profile of v1, /device:TPU:0, one launch (start us, length us, event | category | flops | bytes accessed | tf_op | source)
XLA Modules:
  0.0 50.8 jit_solution(14085658820670353)
XLA Ops:
  0.0 0.8 %reshape.292 = s32[16,512]{1,0:T(8,128)S(1)} reshape(s32[8192]{0:T(1024)} %param.16) | data formatting | bytes 65536 | tf_op jit(solution)/shard_map/reshape | solution.py:14
  0.8 0.7 %copy-done.5 = f32[4,1,128]{2,1,0:T(1,128)S(1)} copy-done((f32[4,1,128]{2,1,0:T(1,128)S(1)}, f32[4,1,128]{2,1,0:T(1,128)}, u32[]{:S(2)}) %copy-start.5) | copy-done | bytes 2072
  1.5 6.2 %all_gather.3 = f32[4,1,512]{2,0,1:T(4,128)S(1)} all-gather(f32[4,1,128]{2,0,1:T(4,128)S(1)} %bitcast.33), channel_id=1, replica_groups=mesh['sky'=4,'tm'=8] {'sky'}, dimensions={2}, use_global_device_ids=true | all-gather | bytes 10240 | tf_op jit(solution)/shard_map/all_gather | solution.py:129
  7.6 22.9 %while.3 = (s32[]{:T(128)}, f32[16,4,512]{2,1,0:T(4,128)S(1)}, s32[16,512]{1,0:T(8,128)S(1)}, f32[16,512]{1,0:T(8,128)S(1)}, f32[4,512]{1,0:T(4,128)S(1)}, /*index=5*/s32[]{:T(128)}) while((s32[]{:T(128)}, f32[16,4,512]{2,1,0:T(4,128)S(1)}, s32[16,512]{1,0:T(8,128)S(1)}, f32[16,512]{1,0:T(8,128)S(1)}, f32[4,512]{1,0:T(4,128)S(1)}, ...), condition=%wide.region_1.2_spmd.clone, body=%wide.region_0.1_spmd.clone.sunk | while | flops 14951938 | bytes 45145 | solution.py:38
  7.6 1.4 %fusion.93 = f32[16,4,512]{2,1,0:T(4,128)S(1)} fusion(f32[16,4,512]{2,1,0:T(4,128)S(1)} %get-tuple-element.186, s32[]{:T(128)S(6)} %copy.36, f32[4,512]{1,0:T(4,128)S(1)} %get-tuple-element.195, f32[512]{0:T(512)S(1)} %get-tuple-element.175, f32[512]{0:T(512)S(1)} %get-tuple-element.176, f32[512]{0:T(512)S(1)} %get-tuple-element.177, ...), kind=kOutput, calls=%fused_computation.2.clone.1 | convolution fusion | flops 14942208 | bytes 26628 | tf_op jit(solution)/shard_map/while/body/eval_jaxpr/dot_general | solution.py:30
  9.1 1.4 %fusion.93 = f32[16,4,512]{2,1,0:T(4,128)S(1)} fusion(f32[16,4,512]{2,1,0:T(4,128)S(1)} %get-tuple-element.186, s32[]{:T(128)S(6)} %copy.36, f32[4,512]{1,0:T(4,128)S(1)} %get-tuple-element.195, f32[512]{0:T(512)S(1)} %get-tuple-element.175, f32[512]{0:T(512)S(1)} %get-tuple-element.176, f32[512]{0:T(512)S(1)} %get-tuple-element.177, ...), kind=kOutput, calls=%fused_computation.2.clone.1 | convolution fusion | flops 14942208 | bytes 26628 | tf_op jit(solution)/shard_map/while/body/eval_jaxpr/dot_general | solution.py:30
  10.5 1.4 %fusion.93 = f32[16,4,512]{2,1,0:T(4,128)S(1)} fusion(f32[16,4,512]{2,1,0:T(4,128)S(1)} %get-tuple-element.186, s32[]{:T(128)S(6)} %copy.36, f32[4,512]{1,0:T(4,128)S(1)} %get-tuple-element.195, f32[512]{0:T(512)S(1)} %get-tuple-element.175, f32[512]{0:T(512)S(1)} %get-tuple-element.176, f32[512]{0:T(512)S(1)} %get-tuple-element.177, ...), kind=kOutput, calls=%fused_computation.2.clone.1 | convolution fusion | flops 14942208 | bytes 26628 | tf_op jit(solution)/shard_map/while/body/eval_jaxpr/dot_general | solution.py:30
  11.9 1.4 %fusion.93 = f32[16,4,512]{2,1,0:T(4,128)S(1)} fusion(f32[16,4,512]{2,1,0:T(4,128)S(1)} %get-tuple-element.186, s32[]{:T(128)S(6)} %copy.36, f32[4,512]{1,0:T(4,128)S(1)} %get-tuple-element.195, f32[512]{0:T(512)S(1)} %get-tuple-element.175, f32[512]{0:T(512)S(1)} %get-tuple-element.176, f32[512]{0:T(512)S(1)} %get-tuple-element.177, ...), kind=kOutput, calls=%fused_computation.2.clone.1 | convolution fusion | flops 14942208 | bytes 26628 | tf_op jit(solution)/shard_map/while/body/eval_jaxpr/dot_general | solution.py:30
  13.4 1.4 %fusion.93 = f32[16,4,512]{2,1,0:T(4,128)S(1)} fusion(f32[16,4,512]{2,1,0:T(4,128)S(1)} %get-tuple-element.186, s32[]{:T(128)S(6)} %copy.36, f32[4,512]{1,0:T(4,128)S(1)} %get-tuple-element.195, f32[512]{0:T(512)S(1)} %get-tuple-element.175, f32[512]{0:T(512)S(1)} %get-tuple-element.176, f32[512]{0:T(512)S(1)} %get-tuple-element.177, ...), kind=kOutput, calls=%fused_computation.2.clone.1 | convolution fusion | flops 14942208 | bytes 26628 | tf_op jit(solution)/shard_map/while/body/eval_jaxpr/dot_general | solution.py:30
  14.8 1.4 %fusion.93 = f32[16,4,512]{2,1,0:T(4,128)S(1)} fusion(f32[16,4,512]{2,1,0:T(4,128)S(1)} %get-tuple-element.186, s32[]{:T(128)S(6)} %copy.36, f32[4,512]{1,0:T(4,128)S(1)} %get-tuple-element.195, f32[512]{0:T(512)S(1)} %get-tuple-element.175, f32[512]{0:T(512)S(1)} %get-tuple-element.176, f32[512]{0:T(512)S(1)} %get-tuple-element.177, ...), kind=kOutput, calls=%fused_computation.2.clone.1 | convolution fusion | flops 14942208 | bytes 26628 | tf_op jit(solution)/shard_map/while/body/eval_jaxpr/dot_general | solution.py:30
  16.2 1.4 %fusion.93 = f32[16,4,512]{2,1,0:T(4,128)S(1)} fusion(f32[16,4,512]{2,1,0:T(4,128)S(1)} %get-tuple-element.186, s32[]{:T(128)S(6)} %copy.36, f32[4,512]{1,0:T(4,128)S(1)} %get-tuple-element.195, f32[512]{0:T(512)S(1)} %get-tuple-element.175, f32[512]{0:T(512)S(1)} %get-tuple-element.176, f32[512]{0:T(512)S(1)} %get-tuple-element.177, ...), kind=kOutput, calls=%fused_computation.2.clone.1 | convolution fusion | flops 14942208 | bytes 26628 | tf_op jit(solution)/shard_map/while/body/eval_jaxpr/dot_general | solution.py:30
  17.7 1.4 %fusion.93 = f32[16,4,512]{2,1,0:T(4,128)S(1)} fusion(f32[16,4,512]{2,1,0:T(4,128)S(1)} %get-tuple-element.186, s32[]{:T(128)S(6)} %copy.36, f32[4,512]{1,0:T(4,128)S(1)} %get-tuple-element.195, f32[512]{0:T(512)S(1)} %get-tuple-element.175, f32[512]{0:T(512)S(1)} %get-tuple-element.176, f32[512]{0:T(512)S(1)} %get-tuple-element.177, ...), kind=kOutput, calls=%fused_computation.2.clone.1 | convolution fusion | flops 14942208 | bytes 26628 | tf_op jit(solution)/shard_map/while/body/eval_jaxpr/dot_general | solution.py:30
  19.1 1.4 %fusion.93 = f32[16,4,512]{2,1,0:T(4,128)S(1)} fusion(f32[16,4,512]{2,1,0:T(4,128)S(1)} %get-tuple-element.186, s32[]{:T(128)S(6)} %copy.36, f32[4,512]{1,0:T(4,128)S(1)} %get-tuple-element.195, f32[512]{0:T(512)S(1)} %get-tuple-element.175, f32[512]{0:T(512)S(1)} %get-tuple-element.176, f32[512]{0:T(512)S(1)} %get-tuple-element.177, ...), kind=kOutput, calls=%fused_computation.2.clone.1 | convolution fusion | flops 14942208 | bytes 26628 | tf_op jit(solution)/shard_map/while/body/eval_jaxpr/dot_general | solution.py:30
  20.5 1.4 %fusion.93 = f32[16,4,512]{2,1,0:T(4,128)S(1)} fusion(f32[16,4,512]{2,1,0:T(4,128)S(1)} %get-tuple-element.186, s32[]{:T(128)S(6)} %copy.36, f32[4,512]{1,0:T(4,128)S(1)} %get-tuple-element.195, f32[512]{0:T(512)S(1)} %get-tuple-element.175, f32[512]{0:T(512)S(1)} %get-tuple-element.176, f32[512]{0:T(512)S(1)} %get-tuple-element.177, ...), kind=kOutput, calls=%fused_computation.2.clone.1 | convolution fusion | flops 14942208 | bytes 26628 | tf_op jit(solution)/shard_map/while/body/eval_jaxpr/dot_general | solution.py:30
  22.0 1.4 %fusion.93 = f32[16,4,512]{2,1,0:T(4,128)S(1)} fusion(f32[16,4,512]{2,1,0:T(4,128)S(1)} %get-tuple-element.186, s32[]{:T(128)S(6)} %copy.36, f32[4,512]{1,0:T(4,128)S(1)} %get-tuple-element.195, f32[512]{0:T(512)S(1)} %get-tuple-element.175, f32[512]{0:T(512)S(1)} %get-tuple-element.176, f32[512]{0:T(512)S(1)} %get-tuple-element.177, ...), kind=kOutput, calls=%fused_computation.2.clone.1 | convolution fusion | flops 14942208 | bytes 26628 | tf_op jit(solution)/shard_map/while/body/eval_jaxpr/dot_general | solution.py:30
  23.4 1.4 %fusion.93 = f32[16,4,512]{2,1,0:T(4,128)S(1)} fusion(f32[16,4,512]{2,1,0:T(4,128)S(1)} %get-tuple-element.186, s32[]{:T(128)S(6)} %copy.36, f32[4,512]{1,0:T(4,128)S(1)} %get-tuple-element.195, f32[512]{0:T(512)S(1)} %get-tuple-element.175, f32[512]{0:T(512)S(1)} %get-tuple-element.176, f32[512]{0:T(512)S(1)} %get-tuple-element.177, ...), kind=kOutput, calls=%fused_computation.2.clone.1 | convolution fusion | flops 14942208 | bytes 26628 | tf_op jit(solution)/shard_map/while/body/eval_jaxpr/dot_general | solution.py:30
  24.8 1.4 %fusion.93 = f32[16,4,512]{2,1,0:T(4,128)S(1)} fusion(f32[16,4,512]{2,1,0:T(4,128)S(1)} %get-tuple-element.186, s32[]{:T(128)S(6)} %copy.36, f32[4,512]{1,0:T(4,128)S(1)} %get-tuple-element.195, f32[512]{0:T(512)S(1)} %get-tuple-element.175, f32[512]{0:T(512)S(1)} %get-tuple-element.176, f32[512]{0:T(512)S(1)} %get-tuple-element.177, ...), kind=kOutput, calls=%fused_computation.2.clone.1 | convolution fusion | flops 14942208 | bytes 26628 | tf_op jit(solution)/shard_map/while/body/eval_jaxpr/dot_general | solution.py:30
  26.3 1.4 %fusion.93 = f32[16,4,512]{2,1,0:T(4,128)S(1)} fusion(f32[16,4,512]{2,1,0:T(4,128)S(1)} %get-tuple-element.186, s32[]{:T(128)S(6)} %copy.36, f32[4,512]{1,0:T(4,128)S(1)} %get-tuple-element.195, f32[512]{0:T(512)S(1)} %get-tuple-element.175, f32[512]{0:T(512)S(1)} %get-tuple-element.176, f32[512]{0:T(512)S(1)} %get-tuple-element.177, ...), kind=kOutput, calls=%fused_computation.2.clone.1 | convolution fusion | flops 14942208 | bytes 26628 | tf_op jit(solution)/shard_map/while/body/eval_jaxpr/dot_general | solution.py:30
  27.7 1.4 %fusion.93 = f32[16,4,512]{2,1,0:T(4,128)S(1)} fusion(f32[16,4,512]{2,1,0:T(4,128)S(1)} %get-tuple-element.186, s32[]{:T(128)S(6)} %copy.36, f32[4,512]{1,0:T(4,128)S(1)} %get-tuple-element.195, f32[512]{0:T(512)S(1)} %get-tuple-element.175, f32[512]{0:T(512)S(1)} %get-tuple-element.176, f32[512]{0:T(512)S(1)} %get-tuple-element.177, ...), kind=kOutput, calls=%fused_computation.2.clone.1 | convolution fusion | flops 14942208 | bytes 26628 | tf_op jit(solution)/shard_map/while/body/eval_jaxpr/dot_general | solution.py:30
  29.1 1.4 %fusion.93 = f32[16,4,512]{2,1,0:T(4,128)S(1)} fusion(f32[16,4,512]{2,1,0:T(4,128)S(1)} %get-tuple-element.186, s32[]{:T(128)S(6)} %copy.36, f32[4,512]{1,0:T(4,128)S(1)} %get-tuple-element.195, f32[512]{0:T(512)S(1)} %get-tuple-element.175, f32[512]{0:T(512)S(1)} %get-tuple-element.176, f32[512]{0:T(512)S(1)} %get-tuple-element.177, ...), kind=kOutput, calls=%fused_computation.2.clone.1 | convolution fusion | flops 14942208 | bytes 26628 | tf_op jit(solution)/shard_map/while/body/eval_jaxpr/dot_general | solution.py:30
  30.5 0.4 multiply_reduce_fusion.1
  31.3 0.7 %copy-done = f32[8192]{0:T(1024)S(1)} copy-done((f32[8192]{0:T(1024)S(1)}, f32[8192]{0:T(1024)}, u32[]{:S(2)}) %copy-start) | copy-done | bytes 32792
  32.0 0.7 %copy-done.1 = f32[8192]{0:T(1024)S(1)} copy-done((f32[8192]{0:T(1024)S(1)}, f32[8192]{0:T(1024)}, u32[]{:S(2)}) %copy-start.1) | copy-done | bytes 32792
  33.0 0.1 stack.66
  33.2 0.1 stack.67
  33.3 0.1 reshape.296
  33.7 0.1 stack.69
  33.9 0.1 stack.70
  34.0 0.1 stack.71
  34.2 0.1 stack.72
  34.4 0.1 stack.73
  34.5 0.1 stack.74
  34.9 0.1 stack.76
  35.1 0.1 stack.77
  35.2 0.1 stack.78
  35.4 0.1 stack.79
  35.6 0.1 stack.80
  35.8 0.1 stack.81
  35.9 0.6 %copy-done.6 = s32[256]{0:T(256)S(1)} copy-done((s32[256]{0:T(256)S(1)}, s32[256]{0:T(256)}, u32[]{:S(2)}) %copy-start.6) | copy-done | bytes 1048
  36.9 0.6 %copy-done.7 = s32[256]{0:T(256)S(1)} copy-done((s32[256]{0:T(256)S(1)}, s32[256]{0:T(256)}, u32[]{:S(2)}) %copy-start.7) | copy-done | bytes 1048
  37.5 0.2 fusion.39
  37.7 2.1 %collective-permute-start = (f32[20,64]{1,0:T(8,128)S(1)}, f32[20,64]{1,0:T(8,128)S(1)}, u32[]{:S(2)}, u32[]{:S(2)}) collective-permute-start(f32[20,64]{1,0:T(8,128)S(1)} %fusion.39), channel_id=1, source_target_pairs={{0,1},{1,0},{2,3},{3,2},{4,5},{5,4},{6,7},{7,6},{8,9},{9,8},{10,11... | collective-permute-start | bytes 15368 | tf_op jit(solution)/shard_map/ppermute | solution.py:140
  39.8 1.7 %collective-permute-done = f32[20,64]{1,0:T(8,128)S(1)} collective-permute-done((f32[20,64]{1,0:T(8,128)S(1)}, f32[20,64]{1,0:T(8,128)S(1)}, u32[]{:S(2)}, u32[]{:S(2)}) %collective-permute-start) | collective-permute-done | bytes 5152 | tf_op jit(solution)/shard_map/ppermute | solution.py:140
  41.5 2.1 %collective-permute-start.1 = (f32[20,64]{1,0:T(8,128)S(1)}, f32[20,64]{1,0:T(8,128)S(1)}, u32[]{:S(2)}, u32[]{:S(2)}) collective-permute-start(f32[20,64]{1,0:T(8,128)S(1)} %add.125), channel_id=1, source_target_pairs={{0,2},{1,3},{2,0},{3,1},{4,6},{5,7},{6,4},{7,5},{8,10},{9,11},{10,... | collective-permute-start | bytes 15368 | tf_op jit(solution)/shard_map/ppermute | solution.py:140
  43.5 1.7 %collective-permute-done.1 = f32[20,64]{1,0:T(8,128)S(1)} collective-permute-done((f32[20,64]{1,0:T(8,128)S(1)}, f32[20,64]{1,0:T(8,128)S(1)}, u32[]{:S(2)}, u32[]{:S(2)}) %collective-permute-start.1) | collective-permute-done | bytes 5152 | tf_op jit(solution)/shard_map/ppermute | solution.py:140
  45.2 3.0 %collective-permute-start.2 = (f32[20,64]{1,0:T(8,128)S(1)}, f32[20,64]{1,0:T(8,128)S(1)}, u32[]{:S(2)}, u32[]{:S(2)}) collective-permute-start(f32[20,64]{1,0:T(8,128)S(1)} %add.126), channel_id=1, source_target_pairs={{0,4},{1,5},{2,6},{3,7},{4,0},{5,1},{6,2},{7,3},{8,12},{9,13},{10,... | collective-permute-start | bytes 15368 | tf_op jit(solution)/shard_map/ppermute | solution.py:140
  48.3 1.7 %collective-permute-done.2 = f32[20,64]{1,0:T(8,128)S(1)} collective-permute-done((f32[20,64]{1,0:T(8,128)S(1)}, f32[20,64]{1,0:T(8,128)S(1)}, u32[]{:S(2)}, u32[]{:S(2)}) %collective-permute-start.2) | collective-permute-done | bytes 5152 | tf_op jit(solution)/shard_map/ppermute | solution.py:140
  50.2 0.6 %stack.83 = f32[5,8]{1,0:T(8,128)} concatenate(f32[1,8]{1,0:T(1,128)S(1)} %get-tuple-element.78, f32[1,8]{1,0:T(1,128)S(1)} %get-tuple-element.79, f32[1,8]{1,0:T(1,128)S(1)} %get-tuple-element.80, f32[1,8]{1,0:T(1,128)S(1)} %get-tuple-element.81, f32[1,8]{1,0:T(1,128)S(1)} %get-tuple-element.82), dimensions={0} | concatenate | bytes 320 | tf_op jit(solution)/shard_map/stack | solution.py:115
  (117 shorter events, 3.0 us)
Async XLA Ops:
  0.0 0.8 %copy-start.3 = (f32[8192]{0:T(1024)S(1)}, f32[8192]{0:T(1024)}, u32[]{:S(2)}) copy-start(f32[8192]{0:T(1024)} %param.15) | copy-start | bytes 98308
  0.8 0.7 %copy-start.5 = (f32[4,1,128]{2,1,0:T(1,128)S(1)}, f32[4,1,128]{2,1,0:T(1,128)}, u32[]{:S(2)}) copy-start(f32[4,1,128]{2,1,0:T(1,128)} %param.11) | copy-start | bytes 6148
  31.2 0.8 %copy-start = (f32[8192]{0:T(1024)S(1)}, f32[8192]{0:T(1024)}, u32[]{:S(2)}) copy-start(f32[8192]{0:T(1024)} %param.12) | copy-start | bytes 98308
  31.2 0.8 %copy-start.2 = (f32[8192]{0:T(1024)S(1)}, f32[8192]{0:T(1024)}, u32[]{:S(2)}) copy-start(f32[8192]{0:T(1024)} %param.14) | copy-start | bytes 98308
  32.0 0.8 %copy-start.1 = (f32[8192]{0:T(1024)S(1)}, f32[8192]{0:T(1024)}, u32[]{:S(2)}) copy-start(f32[8192]{0:T(1024)} %param.13) | copy-start | bytes 98308
  35.9 0.7 %copy-start.6 = (s32[256]{0:T(256)S(1)}, s32[256]{0:T(256)}, u32[]{:S(2)}) copy-start(s32[256]{0:T(256)} %param.18) | copy-start | bytes 3076
  36.8 0.7 %copy-start.7 = (s32[256]{0:T(256)S(1)}, s32[256]{0:T(256)}, u32[]{:S(2)}) copy-start(s32[256]{0:T(256)} %param.17) | copy-start | bytes 3076
  37.7 3.8 %collective-permute-start = (f32[20,64]{1,0:T(8,128)S(1)}, f32[20,64]{1,0:T(8,128)S(1)}, u32[]{:S(2)}, u32[]{:S(2)}) collective-permute-start(f32[20,64]{1,0:T(8,128)S(1)} %fusion.39), channel_id=1, source_target_pairs={{0,1},{1,0},{2,3},{3,2},{4,5},{5,4},{6,7},{7,6},{8,9},{9,8},{10,11... | collective-permute-start | bytes 15368 | tf_op jit(solution)/shard_map/ppermute | solution.py:140
  41.5 3.7 %collective-permute-start.1 = (f32[20,64]{1,0:T(8,128)S(1)}, f32[20,64]{1,0:T(8,128)S(1)}, u32[]{:S(2)}, u32[]{:S(2)}) collective-permute-start(f32[20,64]{1,0:T(8,128)S(1)} %add.125), channel_id=1, source_target_pairs={{0,2},{1,3},{2,0},{3,1},{4,6},{5,7},{6,4},{7,5},{8,10},{9,11},{10,... | collective-permute-start | bytes 15368 | tf_op jit(solution)/shard_map/ppermute | solution.py:140
  45.2 4.7 %collective-permute-start.2 = (f32[20,64]{1,0:T(8,128)S(1)}, f32[20,64]{1,0:T(8,128)S(1)}, u32[]{:S(2)}, u32[]{:S(2)}) collective-permute-start(f32[20,64]{1,0:T(8,128)S(1)} %add.126), channel_id=1, source_target_pairs={{0,4},{1,5},{2,6},{3,7},{4,0},{5,1},{6,2},{7,3},{8,12},{9,13},{10,... | collective-permute-start | bytes 15368 | tf_op jit(solution)/shard_map/ppermute | solution.py:140
  48.3 1.7 %copy-start.4 = (f32[5,8]{1,0:T(8,128)S(1)}, f32[5,8]{1,0:T(8,128)}, u32[]{:S(2)}) copy-start(f32[5,8]{1,0:T(8,128)} %param.19) | copy-start | bytes 484
